TPU v7x, 32 devices: a whole 2x2x4 slice. The times are simulated.
32 devices in a mesh: row: 4 (over x, core), col: 8 (over z, y).
Axes of the slice: x: 2, y: 2, z: 4, core: 2. Of those that a mesh axis runs over, the one named last changes fastest.
Arguments:
- moment_x: float32 [496, 496], P('row', 'col'), may hold values from -8 to 8
- zinv: float32 [496, 496], P('row', 'col'), may hold values from -8 to 8
- positions: int32 [1024, 16], P(('row', 'col')), may hold values from 0 to 495
- entry_count: int32 [1024], P(('row', 'col')), may hold values from 1 to 8
Outputs:
- schur: float32 [1024, 1024], P('row', 'col')
All inputs are finite; a program needn't handle non-finite values.
Results may differ from a plain program's by a relative error of at most 0.0003.
Values sent between devices are 32-bit elements; how exact they have to be, the bound alone decides.
No kernel may reach another device: no remote copies, remote signals or barrier semaphores. Data moves between devices by JAX's collectives and lax.ppermute only.
A program may use at most 64 MiB of HBM per device.

v0:
```python
import jax
import jax.numpy as jnp
from jax import lax
from jax.sharding import PartitionSpec as P


def spread(value, axis, source):
    kept = jnp.where(lax.axis_index(axis) == source, value, 0).astype(value.dtype)
    return lax.psum(kept, axis)


def schur_rows(moment_x, zinv, row_positions, row_counts, col_positions, col_counts, group_rows):
    slot_count = row_positions.shape[1] // 2
    order_size = moment_x.shape[0]
    slot_iota = jnp.arange(slot_count, dtype=jnp.int32)
    whole_iota = jnp.arange(order_size, dtype=jnp.int32)
    col_left = col_positions[:, :slot_count].T.reshape(-1)
    col_right = col_positions[:, slot_count:].T.reshape(-1)
    col_alive = (slot_iota[:, None] < col_counts[None, :]).astype(jnp.float32).reshape(-1)
    pick_left = jnp.where(whole_iota[:, None] == col_left[None, :], col_alive[None, :], 0.0)
    pick_right = (whole_iota[:, None] == col_right[None, :]).astype(jnp.float32)
    ncols = col_positions.shape[0]
    nrows = row_positions.shape[0]

    def one_group(packed):
        grp_positions, grp_counts = packed
        grp_left = grp_positions[:, :slot_count].reshape(-1)
        grp_right = grp_positions[:, slot_count:].reshape(-1)
        grp_alive = (slot_iota[None, :] < grp_counts[:, None]).astype(jnp.float32).reshape(-1)
        x_rows = jnp.take(moment_x, grp_right, axis=0)
        w_rows = jnp.take(zinv, grp_left, axis=0)
        x_picked = jnp.dot(
            x_rows, pick_left, preferred_element_type=jnp.float32, precision=lax.Precision.HIGHEST
        )
        w_picked = jnp.dot(
            w_rows, pick_right, preferred_element_type=jnp.float32, precision=lax.Precision.HIGHEST
        )
        terms = x_picked * w_picked * grp_alive[:, None]
        return jnp.sum(terms.reshape(group_rows, slot_count, slot_count, ncols), axis=(1, 2))

    grouped = (
        row_positions.reshape(nrows // group_rows, group_rows, 2 * slot_count),
        row_counts.reshape(nrows // group_rows, group_rows),
    )
    return lax.map(one_group, grouped).reshape(nrows, ncols)


def collect(pieces):
    wide = (
        lax.all_gather(pieces[0], "col", axis=1, tiled=True),
        lax.all_gather(pieces[1], "col", axis=1, tiled=True),
    )
    return (
        lax.all_gather(wide[0], "row", axis=0, tiled=True),
        lax.all_gather(wide[1], "row", axis=0, tiled=True),
    )


def shards(moment_x, zinv, positions, entry_count):
    full_x, full_w = collect((moment_x, zinv))
    row_positions, row_counts = (
        lax.all_gather(positions, "col", axis=0, tiled=True),
        lax.all_gather(entry_count, "col", axis=0, tiled=True),
    )
    col_devices = lax.axis_size("col")
    share_ratio = col_devices // lax.axis_size("row")
    col_index = lax.axis_index("col")
    piece_size = row_counts.shape[0] // share_ratio
    offset_rows = col_index % share_ratio * piece_size
    piece_positions = lax.dynamic_slice_in_dim(row_positions, offset_rows, piece_size, 0)
    piece_counts = lax.dynamic_slice_in_dim(row_counts, offset_rows, piece_size, 0)
    col_positions, col_counts = (
        spread(piece_positions, "row", col_index // share_ratio),
        spread(piece_counts, "row", col_index // share_ratio),
    )
    group_rows = min(64, row_counts.shape[0])
    return schur_rows(
        full_x, full_w, row_positions, row_counts, col_positions, col_counts, group_rows
    )


def solution(mesh):
    return jax.shard_map(
        shards,
        mesh=mesh,
        in_specs=(P("row", "col"), P("row", "col"), P(("row", "col"), None), P(("row", "col"))),
        out_specs=P("row", "col"),
        check_vma=False,
    )
```

profile of v0, /device:TPU:0, one launch (start us, length us, event | category | flops | bytes accessed | tf_op | source)
XLA Modules:
  0.0 191.0 jit_solution(2002128787792000203)
XLA Ops:
  0.0 32.5 %all-gather = s32[8,32,16]{1,2,0:T(8,128)S(1)} all-gather(s32[1,32,16]{1,2,0:T(8,128)} %bitcast.49), channel_id=1, replica_groups=mesh['row'=4,'col'=8] {'col'}, dimensions={0}, use_global_device_ids=true | all-gather | bytes 18432 | tf_op jit(solution)/shard_map/all_gather | solution.py:62
  32.7 1.3 dynamic-slice
  34.7 0.9 dynamic-update-slice
  35.6 10.8 %all-reduce = s32[256]{0:T(256)S(1)} all-reduce(s32[256]{0:T(256)S(1)} %dynamic-update-slice), channel_id=1, replica_groups=mesh['row'=4,'col'=8] {'col'}, use_global_device_ids=true, to_apply=%add | all-reduce | flops 256 | bytes 2048
  46.4 5.0 %all-reduce.1 = (s32[128,16]{0,1:T(8,128)S(1)}, s32[128]{0:T(128)S(1)}) all-reduce(s32[128,16]{0,1:T(8,128)S(1)} %dynamic-slice_select_fusion, s32[128]{0:T(128)S(1)} %broadcast_select_fusion), channel_id=1, replica_groups=mesh['row'=4,'col'=8] {'row'}, use_global_device_ids=true, to_apply=%region_0.1 | all-reduce | flops 2176 | bytes 17408 | tf_op jit(solution)/shard_map/psum | solution.py:9
  51.7 31.1 %all-gather.1 = f32[8,62,124]{2,1,0:T(8,128)S(1)} all-gather(f32[1,62,124]{2,1,0:T(8,128)} %bitcast.47), channel_id=1, replica_groups=mesh['row'=4,'col'=8] {'col'}, dimensions={0}, use_global_device_ids=true | all-gather | bytes 276768 | tf_op jit(solution)/shard_map/all_gather | solution.py:50
  82.8 9.1 %all-gather.2 = f32[4,124,496]{1,2,0:T(8,128)S(1)} all-gather(f32[1,124,496]{1,2,0:T(8,128)S(1)} %bitcast.44), channel_id=1, replica_groups=mesh['row'=4,'col'=8] {'row'}, dimensions={0}, use_global_device_ids=true | all-gather | bytes 1230080 | tf_op jit(solution)/shard_map/all_gather | solution.py:54
  91.9 0.4 copy.13
  92.2 0.1 reshape.95
  92.4 0.3 copy-done
  92.6 30.7 %all-gather.3 = f32[8,62,124]{2,1,0:T(8,128)S(1)} all-gather(f32[1,62,124]{2,1,0:T(8,128)S(1)} %bitcast.48), channel_id=1, replica_groups=mesh['row'=4,'col'=8] {'col'}, dimensions={0}, use_global_device_ids=true | all-gather | bytes 276768 | tf_op jit(solution)/shard_map/all_gather | solution.py:51
  123.4 9.6 %all-gather.4 = f32[4,124,496]{1,2,0:T(8,128)S(1)} all-gather(f32[1,124,496]{1,2,0:T(8,128)S(1)} %bitcast.45), channel_id=1, replica_groups=mesh['row'=4,'col'=8] {'row'}, dimensions={0}, use_global_device_ids=true | all-gather | bytes 1230080 | tf_op jit(solution)/shard_map/all_gather | solution.py:55
  133.0 0.4 copy.14
  133.4 0.1 reshape.99
  133.5 56.9 %while.11 = (s32[]{:T(128)}, f32[4,64,128]{2,1,0:T(8,128)S(1)}, s32[4,64,16]{2,1,0:T(8,128)S(1)}, f32[496,496]{1,0:T(8,128)S(1)}, f32[496,496]{1,0:T(8,128)S(1)}...) while((s32[]{:T(128)}, f32[4,64,128]{2,1,0:T(8,128)S(1)}, ...), condition=%wide.region_4.6_spmd.clone, body=%wide.region_2.5_spmd.clone.sunk | while | flops 6245240832 | bytes 10464113 | solution.py:45
  133.7 1.6 gather_fusion
  135.4 5.0 %fusion.41 = f32[512,1024]{1,0:T(8,128)} fusion(f32[512,496]{1,0:T(8,128)S(1)} %gather_fusion, s32[1024]{0:T(1024)S(1)} %get-tuple-element.208, pred[512]{0:T(512)(128)(4,1)S(1)} %compare_and_fusion.4), kind=kOutput, calls=%fused_computation.6.clone.1 | convolution fusion | flops 3121831936 | bytes 3117568 | tf_op jit(solution)/shard_map/while/body/eval_jaxpr/dot_general | solution.py:35
  140.5 1.6 gather_fusion.1
  142.3 5.4 %bitcast_reduce_fusion.2 = f32[64,128]{1,0:T(8,128)S(1)} fusion(f32[512,1024]{1,0:T(8,128)} %fusion.41, f32[512,496]{1,0:T(8,128)S(1)} %gather_fusion.1, f32[512]{0:T(512)S(1)} %reshape.124, f32[1024]{0:T(1024)S(1)} %get-tuple-element.207, s32[1024]{0:T(1024)S(1)} %get-tuple-element.206, pred[512]{0:T(512)(128)(4,1)S(1)} %compare_and_fusion.5), kind=kOutput, calls=%fused_computation.5.clone.1 | convolution fusion | flops 3123396608 | bytes 3156480 | tf_op jit(solution)/shard_map/while/body/eval_jaxpr/dot_general | solution.py:32
  147.9 1.6 gather_fusion
  149.6 5.0 %fusion.41 = f32[512,1024]{1,0:T(8,128)} fusion(f32[512,496]{1,0:T(8,128)S(1)} %gather_fusion, s32[1024]{0:T(1024)S(1)} %get-tuple-element.208, pred[512]{0:T(512)(128)(4,1)S(1)} %compare_and_fusion.4), kind=kOutput, calls=%fused_computation.6.clone.1 | convolution fusion | flops 3121831936 | bytes 3117568 | tf_op jit(solution)/shard_map/while/body/eval_jaxpr/dot_general | solution.py:35
  154.7 1.6 gather_fusion.1
  156.6 5.4 %bitcast_reduce_fusion.2 = f32[64,128]{1,0:T(8,128)S(1)} fusion(f32[512,1024]{1,0:T(8,128)} %fusion.41, f32[512,496]{1,0:T(8,128)S(1)} %gather_fusion.1, f32[512]{0:T(512)S(1)} %reshape.124, f32[1024]{0:T(1024)S(1)} %get-tuple-element.207, s32[1024]{0:T(1024)S(1)} %get-tuple-element.206, pred[512]{0:T(512)(128)(4,1)S(1)} %compare_and_fusion.5), kind=kOutput, calls=%fused_computation.5.clone.1 | convolution fusion | flops 3123396608 | bytes 3156480 | tf_op jit(solution)/shard_map/while/body/eval_jaxpr/dot_general | solution.py:32
  162.2 1.6 gather_fusion
  163.8 5.0 %fusion.41 = f32[512,1024]{1,0:T(8,128)} fusion(f32[512,496]{1,0:T(8,128)S(1)} %gather_fusion, s32[1024]{0:T(1024)S(1)} %get-tuple-element.208, pred[512]{0:T(512)(128)(4,1)S(1)} %compare_and_fusion.4), kind=kOutput, calls=%fused_computation.6.clone.1 | convolution fusion | flops 3121831936 | bytes 3117568 | tf_op jit(solution)/shard_map/while/body/eval_jaxpr/dot_general | solution.py:35
  168.9 1.6 gather_fusion.1
  170.8 5.4 %bitcast_reduce_fusion.2 = f32[64,128]{1,0:T(8,128)S(1)} fusion(f32[512,1024]{1,0:T(8,128)} %fusion.41, f32[512,496]{1,0:T(8,128)S(1)} %gather_fusion.1, f32[512]{0:T(512)S(1)} %reshape.124, f32[1024]{0:T(1024)S(1)} %get-tuple-element.207, s32[1024]{0:T(1024)S(1)} %get-tuple-element.206, pred[512]{0:T(512)(128)(4,1)S(1)} %compare_and_fusion.5), kind=kOutput, calls=%fused_computation.5.clone.1 | convolution fusion | flops 3123396608 | bytes 3156480 | tf_op jit(solution)/shard_map/while/body/eval_jaxpr/dot_general | solution.py:32
  176.4 1.6 gather_fusion
  178.0 5.0 %fusion.41 = f32[512,1024]{1,0:T(8,128)} fusion(f32[512,496]{1,0:T(8,128)S(1)} %gather_fusion, s32[1024]{0:T(1024)S(1)} %get-tuple-element.208, pred[512]{0:T(512)(128)(4,1)S(1)} %compare_and_fusion.4), kind=kOutput, calls=%fused_computation.6.clone.1 | convolution fusion | flops 3121831936 | bytes 3117568 | tf_op jit(solution)/shard_map/while/body/eval_jaxpr/dot_general | solution.py:35
  183.2 1.6 gather_fusion.1
  185.0 5.4 %bitcast_reduce_fusion.2 = f32[64,128]{1,0:T(8,128)S(1)} fusion(f32[512,1024]{1,0:T(8,128)} %fusion.41, f32[512,496]{1,0:T(8,128)S(1)} %gather_fusion.1, f32[512]{0:T(512)S(1)} %reshape.124, f32[1024]{0:T(1024)S(1)} %get-tuple-element.207, s32[1024]{0:T(1024)S(1)} %get-tuple-element.206, pred[512]{0:T(512)(128)(4,1)S(1)} %compare_and_fusion.5), kind=kOutput, calls=%fused_computation.5.clone.1 | convolution fusion | flops 3123396608 | bytes 3156480 | tf_op jit(solution)/shard_map/while/body/eval_jaxpr/dot_general | solution.py:32
  190.4 0.6 copy-done.1
  (70 shorter events, 2.4 us)
Async XLA Ops:
  91.9 0.8 copy-start
  190.4 0.7 copy-start.1
where the time goes:
time: 191 us
  blocking collectives  129 us (68%)
  matrix products  41.5 us (22%)
  local copies, waits for them, and re-layouts  18.8 us (10%)
    all_gather x1, blocking collectives, shards(): lax.all_gather(positions, 'col', axis=0, tiled=True)  32.5 us
    all_gather x1, blocking collectives, collect(): lax.all_gather(pieces[0], 'col', axis=1, tiled=True)  31.1 us
    all_gather x1, blocking collectives, collect(): lax.all_gather(pieces[1], 'col', axis=1, tiled=True)  30.7 us
    dot_general x4, matrix products, one_group(): jnp.dot(x_rows, pick_left, preferred_element_type=jnp.float32, precision=...  21.4 us
    dot_general x4, matrix products, one_group(): jnp.dot(w_rows, pick_right, preferred_element_type=jnp.float32, precision...  20.1 us
    unnamed x1, blocking collectives  10.8 us
    all_gather x1, blocking collectives, collect(): lax.all_gather(wide[1], 'row', axis=0, tiled=True)  9.63 us
    all_gather x1, blocking collectives, collect(): lax.all_gather(wide[0], 'row', axis=0, tiled=True)  9.1 us

commit v1 on v0

--- a/solution.py
+++ b/solution.py
@@ -48,7 +48,7 @@
 def collect(pieces):
     wide = (
         lax.all_gather(pieces[0], "col", axis=1, tiled=True),
-        lax.all_gather(pieces[1], "col", axis=1, tiled=True),
+        jnp.concatenate(lax.all_gather(pieces[1], "col"), axis=1),
     )
     return (
         lax.all_gather(wide[0], "row", axis=0, tiled=True),

time: 191 us -> 191 us (level)
  no operation moved by 1% of the time
where the time goes in v1:
time: 191 us
  blocking collectives  129 us (68%)
  matrix products  41.5 us (22%)
  local copies, waits for them, and re-layouts  18.8 us (10%)
    all_gather x1, blocking collectives, shards(): lax.all_gather(positions, 'col', axis=0, tiled=True)  32.5 us
    all_gather x1, blocking collectives, collect(): lax.all_gather(pieces[0], 'col', axis=1, tiled=True)  31.1 us
    all_gather x1, blocking collectives, collect(): lax.all_gather(pieces[1], 'col')  30.7 us
    dot_general x4, matrix products, one_group(): jnp.dot(x_rows, pick_left, preferred_element_type=jnp.float32, precision=...  21.4 us
    dot_general x4, matrix products, one_group(): jnp.dot(w_rows, pick_right, preferred_element_type=jnp.float32, precision...  20.1 us
    unnamed x1, blocking collectives  10.8 us
    all_gather x1, blocking collectives, collect(): lax.all_gather(wide[1], 'row', axis=0, tiled=True)  9.63 us
    all_gather x1, blocking collectives, collect(): lax.all_gather(wide[0], 'row', axis=0, tiled=True)  9.1 us

profile of v1, /device:TPU:0, one launch (start us, length us, event | category | flops | bytes accessed | tf_op | source)
XLA Modules:
  0.0 191.0 jit_solution(2002128787792000203)
XLA Ops:
  0.0 32.5 %all-gather.1 = s32[8,32,16]{1,2,0:T(8,128)S(1)} all-gather(s32[1,32,16]{1,2,0:T(8,128)} %bitcast.47), channel_id=1, replica_groups=mesh['row'=4,'col'=8] {'col'}, dimensions={0}, use_global_device_ids=true | all-gather | bytes 18432 | tf_op jit(solution)/shard_map/all_gather | solution.py:62
  32.7 1.3 dynamic-slice
  34.7 0.9 dynamic-update-slice
  35.6 10.8 %all-reduce = s32[256]{0:T(256)S(1)} all-reduce(s32[256]{0:T(256)S(1)} %dynamic-update-slice), channel_id=1, replica_groups=mesh['row'=4,'col'=8] {'col'}, use_global_device_ids=true, to_apply=%add | all-reduce | flops 256 | bytes 2048
  46.4 5.0 %all-reduce.1 = (s32[128,16]{0,1:T(8,128)S(1)}, s32[128]{0:T(128)S(1)}) all-reduce(s32[128,16]{0,1:T(8,128)S(1)} %dynamic-slice_select_fusion, s32[128]{0:T(128)S(1)} %broadcast_select_fusion), channel_id=1, replica_groups=mesh['row'=4,'col'=8] {'row'}, use_global_device_ids=true, to_apply=%region_0.1 | all-reduce | flops 2176 | bytes 17408 | tf_op jit(solution)/shard_map/psum | solution.py:9
  51.7 31.1 %all-gather.2 = f32[8,62,124]{2,1,0:T(8,128)S(1)} all-gather(f32[1,62,124]{2,1,0:T(8,128)} %bitcast.45), channel_id=1, replica_groups=mesh['row'=4,'col'=8] {'col'}, dimensions={0}, use_global_device_ids=true | all-gather | bytes 276768 | tf_op jit(solution)/shard_map/all_gather | solution.py:50
  82.8 9.1 %all-gather.3 = f32[4,124,496]{1,2,0:T(8,128)S(1)} all-gather(f32[1,124,496]{1,2,0:T(8,128)S(1)} %bitcast.43), channel_id=1, replica_groups=mesh['row'=4,'col'=8] {'row'}, dimensions={0}, use_global_device_ids=true | all-gather | bytes 1230080 | tf_op jit(solution)/shard_map/all_gather | solution.py:54
  91.9 0.4 copy.13
  92.2 0.1 reshape.104
  92.4 0.3 copy-done
  92.6 30.7 %all-gather.4 = f32[8,124,62]{1,2,0:T(8,128)S(1)} all-gather(f32[1,124,62]{1,2,0:T(8,128)S(1)} %bitcast.46), channel_id=2, replica_groups=mesh['row'=4,'col'=8] {'col'}, dimensions={0}, use_global_device_ids=true | all-gather | bytes 276768 | tf_op jit(solution)/shard_map/all_gather | solution.py:51
  123.4 9.6 %all-gather.5 = f32[4,124,496]{1,2,0:T(8,128)S(1)} all-gather(f32[1,124,496]{1,2,0:T(8,128)S(1)} %reshape.107), channel_id=1, replica_groups=mesh['row'=4,'col'=8] {'row'}, dimensions={0}, use_global_device_ids=true | all-gather | bytes 1230080 | tf_op jit(solution)/shard_map/all_gather | solution.py:55
  133.0 0.4 copy.14
  133.4 0.1 reshape.108
  133.5 56.9 %while.11 = (s32[]{:T(128)}, f32[4,64,128]{2,1,0:T(8,128)S(1)}, s32[4,64,16]{2,1,0:T(8,128)S(1)}, f32[496,496]{1,0:T(8,128)S(1)}, f32[496,496]{1,0:T(8,128)S(1)}...) while((s32[]{:T(128)}, f32[4,64,128]{2,1,0:T(8,128)S(1)}, ...), condition=%wide.region_4.6_spmd.clone, body=%wide.region_2.5_spmd.clone.sunk | while | flops 6245240832 | bytes 10464113 | solution.py:45
  133.7 1.6 gather_fusion
  135.4 5.0 %fusion.41 = f32[512,1024]{1,0:T(8,128)} fusion(f32[512,496]{1,0:T(8,128)S(1)} %gather_fusion, s32[1024]{0:T(1024)S(1)} %get-tuple-element.208, pred[512]{0:T(512)(128)(4,1)S(1)} %compare_and_fusion.4), kind=kOutput, calls=%fused_computation.6.clone.1 | convolution fusion | flops 3121831936 | bytes 3117568 | tf_op jit(solution)/shard_map/while/body/eval_jaxpr/dot_general | solution.py:35
  140.5 1.6 gather_fusion.1
  142.3 5.4 %bitcast_reduce_fusion.2 = f32[64,128]{1,0:T(8,128)S(1)} fusion(f32[512,1024]{1,0:T(8,128)} %fusion.41, f32[512,496]{1,0:T(8,128)S(1)} %gather_fusion.1, f32[512]{0:T(512)S(1)} %reshape.135, f32[1024]{0:T(1024)S(1)} %get-tuple-element.207, s32[1024]{0:T(1024)S(1)} %get-tuple-element.206, pred[512]{0:T(512)(128)(4,1)S(1)} %compare_and_fusion.5), kind=kOutput, calls=%fused_computation.5.clone.1 | convolution fusion | flops 3123396608 | bytes 3156480 | tf_op jit(solution)/shard_map/while/body/eval_jaxpr/dot_general | solution.py:32
  147.9 1.6 gather_fusion
  149.6 5.0 %fusion.41 = f32[512,1024]{1,0:T(8,128)} fusion(f32[512,496]{1,0:T(8,128)S(1)} %gather_fusion, s32[1024]{0:T(1024)S(1)} %get-tuple-element.208, pred[512]{0:T(512)(128)(4,1)S(1)} %compare_and_fusion.4), kind=kOutput, calls=%fused_computation.6.clone.1 | convolution fusion | flops 3121831936 | bytes 3117568 | tf_op jit(solution)/shard_map/while/body/eval_jaxpr/dot_general | solution.py:35
  154.7 1.6 gather_fusion.1
  156.6 5.4 %bitcast_reduce_fusion.2 = f32[64,128]{1,0:T(8,128)S(1)} fusion(f32[512,1024]{1,0:T(8,128)} %fusion.41, f32[512,496]{1,0:T(8,128)S(1)} %gather_fusion.1, f32[512]{0:T(512)S(1)} %reshape.135, f32[1024]{0:T(1024)S(1)} %get-tuple-element.207, s32[1024]{0:T(1024)S(1)} %get-tuple-element.206, pred[512]{0:T(512)(128)(4,1)S(1)} %compare_and_fusion.5), kind=kOutput, calls=%fused_computation.5.clone.1 | convolution fusion | flops 3123396608 | bytes 3156480 | tf_op jit(solution)/shard_map/while/body/eval_jaxpr/dot_general | solution.py:32
  162.2 1.6 gather_fusion
  163.8 5.0 %fusion.41 = f32[512,1024]{1,0:T(8,128)} fusion(f32[512,496]{1,0:T(8,128)S(1)} %gather_fusion, s32[1024]{0:T(1024)S(1)} %get-tuple-element.208, pred[512]{0:T(512)(128)(4,1)S(1)} %compare_and_fusion.4), kind=kOutput, calls=%fused_computation.6.clone.1 | convolution fusion | flops 3121831936 | bytes 3117568 | tf_op jit(solution)/shard_map/while/body/eval_jaxpr/dot_general | solution.py:35
  168.9 1.6 gather_fusion.1
  170.8 5.4 %bitcast_reduce_fusion.2 = f32[64,128]{1,0:T(8,128)S(1)} fusion(f32[512,1024]{1,0:T(8,128)} %fusion.41, f32[512,496]{1,0:T(8,128)S(1)} %gather_fusion.1, f32[512]{0:T(512)S(1)} %reshape.135, f32[1024]{0:T(1024)S(1)} %get-tuple-element.207, s32[1024]{0:T(1024)S(1)} %get-tuple-element.206, pred[512]{0:T(512)(128)(4,1)S(1)} %compare_and_fusion.5), kind=kOutput, calls=%fused_computation.5.clone.1 | convolution fusion | flops 3123396608 | bytes 3156480 | tf_op jit(solution)/shard_map/while/body/eval_jaxpr/dot_general | solution.py:32
  176.4 1.6 gather_fusion
  178.0 5.0 %fusion.41 = f32[512,1024]{1,0:T(8,128)} fusion(f32[512,496]{1,0:T(8,128)S(1)} %gather_fusion, s32[1024]{0:T(1024)S(1)} %get-tuple-element.208, pred[512]{0:T(512)(128)(4,1)S(1)} %compare_and_fusion.4), kind=kOutput, calls=%fused_computation.6.clone.1 | convolution fusion | flops 3121831936 | bytes 3117568 | tf_op jit(solution)/shard_map/while/body/eval_jaxpr/dot_general | solution.py:35
  183.2 1.6 gather_fusion.1
  185.0 5.4 %bitcast_reduce_fusion.2 = f32[64,128]{1,0:T(8,128)S(1)} fusion(f32[512,1024]{1,0:T(8,128)} %fusion.41, f32[512,496]{1,0:T(8,128)S(1)} %gather_fusion.1, f32[512]{0:T(512)S(1)} %reshape.135, f32[1024]{0:T(1024)S(1)} %get-tuple-element.207, s32[1024]{0:T(1024)S(1)} %get-tuple-element.206, pred[512]{0:T(512)(128)(4,1)S(1)} %compare_and_fusion.5), kind=kOutput, calls=%fused_computation.5.clone.1 | convolution fusion | flops 3123396608 | bytes 3156480 | tf_op jit(solution)/shard_map/while/body/eval_jaxpr/dot_general | solution.py:32
  190.4 0.6 copy-done.1
  (70 shorter events, 2.4 us)
Async XLA Ops:
  91.9 0.8 copy-start
  190.4 0.7 copy-start.1
